TPU v7x, 32 devices: a whole 2x2x4 slice. The times are simulated.
32 devices in a mesh: seq: 8 (over z, core), tp: 4 (over y, x).
Axes of the slice: x: 2, y: 2, z: 4, core: 2. Of those that a mesh axis runs over, the one named last changes fastest.
Arguments:
- queries: bfloat16 [8192, 4096], P(('seq', 'tp')), may hold values from -170 to 170, as said below
- keys: bfloat16 [8192, 512], P(('seq', 'tp')), may hold values from -6 to 6
- values: bfloat16 [8192, 512], P(('seq', 'tp')), may hold values from -6 to 6
- segments: int32 [8192], replicated, may hold values from 0 to 63, never falling along the last dimension, each value on 1 to 256 neighbouring positions
- out_weight: bfloat16 [4096, 4096], P('tp'), may hold values from -0.75 to 0.75
Outputs:
- mixed: bfloat16 [8192, 4096], P(('seq', 'tp'))
Inputs may be any that keep to these rules, and one draw needn't show every extreme that they name: `segments`: document ids never fall along the positions; one document holds at most 256 positions. `queries`: independent entries.
All inputs are finite; a program needn't handle non-finite values.
Results may differ from a plain program's by a relative error of at most 0.014.
Values may be sent and summed in bfloat16 or wider, within the bound.
A program may use at most 64 MiB of HBM per device.

v0:
```python
import jax
import jax.numpy as jnp
from jax import lax
from jax.sharding import PartitionSpec as P

KVH = 4
HD = 128
DOC = 256


def from_behind(value, axis, steps):
    count = lax.axis_size(axis)
    first, last = (max(0, -steps), min(count, count - steps))
    return lax.ppermute(value, axis, [(source, source + steps) for source in range(first, last)])


def spread_heads(source, copies):
    if copies == 1:
        return source
    rows = source.shape[0]
    widened = jnp.repeat(source.reshape(rows, KVH, HD), copies, axis=1)
    return widened.reshape(rows, KVH * copies * HD)


def shards(queries, keys, values, segments, out_weight):
    tp_count = lax.axis_size("tp")
    copies = max(tp_count // KVH, 1)
    tile_rows = DOC // 2
    inverse_root = HD ** (-0.5)
    keys_wide = spread_heads(keys, copies)
    values_wide = spread_heads(values, copies)
    local_queries, local_keys, local_values = (
        lax.all_to_all(queries, "tp", split_axis=1, concat_axis=0, tiled=True),
        lax.all_to_all(keys_wide, "tp", split_axis=1, concat_axis=0, tiled=True),
        lax.all_to_all(values_wide, "tp", split_axis=1, concat_axis=0, tiled=True),
    )
    row_count = local_queries.shape[0]
    kv_local = local_keys.shape[1] // HD
    query_local = local_queries.shape[1] // HD
    local_group = query_local // kv_local
    tile_count = row_count // tile_rows
    first_row = lax.axis_index("seq") * row_count
    closing = jnp.stack([local_keys[row_count - DOC :], local_values[row_count - DOC :]])
    earlier = from_behind(closing, "seq", 1)
    key_ext = jnp.concatenate([earlier[0], local_keys], 0).reshape(row_count + DOC, kv_local, HD)
    value_ext = jnp.concatenate([earlier[1], local_values], 0).reshape(
        row_count + DOC, kv_local, HD
    )
    padded_seg = jnp.concatenate([jnp.full((DOC,), -1, jnp.int32), segments], 0)
    key_seg = lax.dynamic_slice_in_dim(padded_seg, first_row, row_count + DOC)
    query_seg = key_seg[DOC:].reshape(tile_count, tile_rows)
    key_pos = first_row - DOC + jnp.arange(row_count + DOC, dtype=jnp.int32)
    query_pos = (first_row + jnp.arange(row_count, dtype=jnp.int32)).reshape(tile_count, tile_rows)

    def windows(source):
        blocks = source.reshape((tile_count + 2, tile_rows) + source.shape[1:])
        return jnp.concatenate([blocks[:-2], blocks[1:-1], blocks[2:]], 1)

    key_win = windows(key_ext)
    value_win = windows(value_ext)
    pos_win = windows(key_pos)
    seg_win = windows(key_seg)
    query_tiles = local_queries.reshape(tile_count, tile_rows, kv_local, local_group, HD)
    allowed = (pos_win[:, None, :] <= query_pos[:, :, None]) & (
        seg_win[:, None, :] == query_seg[:, :, None]
    )
    allowed = allowed[:, None, None]
    scores = (
        jnp.einsum("ctkgd,cskd->ckgts", query_tiles, key_win, preferred_element_type=jnp.float32)
        * inverse_root
    )
    masked = jnp.where(allowed, scores, jnp.float32(-1e30))
    top_score = jnp.max(masked, axis=-1, keepdims=True)
    weights = jnp.where(allowed, jnp.exp(masked - top_score), jnp.float32(0.0))
    denominator = jnp.sum(weights, axis=-1)
    totals = jnp.einsum(
        "ckgts,cskd->ckgtd",
        weights.astype(jnp.bfloat16),
        value_win,
        preferred_element_type=jnp.float32,
    )
    attended = (totals / denominator[..., None]).astype(jnp.bfloat16)
    attended = jnp.transpose(attended, (0, 3, 1, 2, 4)).reshape(row_count, query_local * HD)
    return lax.psum_scatter(
        jnp.dot(attended, out_weight, preferred_element_type=jnp.float32).astype(jnp.bfloat16),
        "tp",
        scatter_dimension=0,
        tiled=True,
    )


def solution(mesh):
    placed = (
        P(("seq", "tp"), None),
        P(("seq", "tp"), None),
        P(("seq", "tp"), None),
        P(),
        P("tp", None),
    )
    return jax.shard_map(
        shards, mesh=mesh, in_specs=placed, out_specs=P(("seq", "tp"), None), check_vma=False
    )
```

profile of v0, /device:TPU:0, one launch (start us, length us, event | category | flops | bytes accessed | tf_op | source)
XLA Modules:
  0.0 175.0 jit_solution(6000773762197747919)
XLA Ops:
  6.5 0.0 copy-start
  6.5 0.0 copy-start.2
  6.5 0.9 copy-done
  7.5 0.7 copy_bitcast_fusion.2
  8.2 5.2 %all-to-all-start = ((bf16[256,4,128]{2,0,1:T(8,128)(2,1)}), bf16[256,4,128]{2,0,1:T(8,128)(2,1)S(1)}, u32[]{:S(2)}, u32[]{:S(2)}) async-start(bf16[256,4,128]{2,0,1:T(8,128)(2,1)} %copy_bitcast_fusion.2), calls=%async_computation | async-start | bytes 524288 | tf_op jit(solution)/shard_map/all_to_all | solution.py:34
  13.4 1.7 copy_bitcast_fusion.1
  15.1 3.7 %all-to-all-done = bf16[256,4,128]{2,0,1:T(8,128)(2,1)S(1)} async-done(((bf16[256,4,128]{2,0,1:T(8,128)(2,1)}), bf16[256,4,128]{2,0,1:T(8,128)(2,1)S(1)}, u32[]{:S(2)}, u32[]{:S(2)}) %all-to-all-start) | async-done | bytes 262176 | tf_op jit(solution)/shard_map/all_to_all | solution.py:34
  18.8 3.4 %all-to-all-start.1 = ((bf16[256,4,128]{2,0,1:T(8,128)(2,1)}), bf16[256,4,128]{2,0,1:T(8,128)(2,1)S(1)}, u32[]{:S(2)}, u32[]{:S(2)}) async-start(bf16[256,4,128]{2,0,1:T(8,128)(2,1)} %copy_bitcast_fusion.1), calls=%async_computation.1 | async-start | bytes 524288 | tf_op jit(solution)/shard_map/all_to_all | solution.py:35
  22.2 3.1 %copy.34 = bf16[32,4,8,1024]{3,2,0,1:T(8,128)(2,1)} copy(bf16[32,4,8,1024]{3,2,1,0:T(8,128)(2,1)} %bitcast.91) | data formatting | bytes 4194304 | tf_op jit(solution)/shard_map/all_to_all | solution.py:33
  25.3 2.2 %all-to-all-done.1 = bf16[256,4,128]{2,0,1:T(8,128)(2,1)S(1)} async-done(((bf16[256,4,128]{2,0,1:T(8,128)(2,1)}), bf16[256,4,128]{2,0,1:T(8,128)(2,1)S(1)}, u32[]{:S(2)}, u32[]{:S(2)}) %all-to-all-start.1) | async-done | bytes 262176 | tf_op jit(solution)/shard_map/all_to_all | solution.py:35
  27.6 3.6 %all-to-all-start.2 = ((bf16[256,4,1024]{2,0,1:T(8,128)(2,1)}), bf16[256,4,1024]{2,0,1:T(8,128)(2,1)S(1)}, u32[]{:S(2)}, u32[]{:S(2)}) async-start(bf16[256,4,1024]{2,0,1:T(8,128)(2,1)} %bitcast.89), calls=%async_computation.2 | async-start | bytes 4194304 | tf_op jit(solution)/shard_map/all_to_all | solution.py:33
  31.2 0.0 reduce-scatter.2.cloned.1.call-start
  31.2 0.0 copy-done.2
  31.3 0.1 fusion.25
  31.4 1.3 collective-permute-start
  32.7 1.2 compare_and_fusion
  33.9 0.0 collective-permute-done
  33.9 0.9 fusion.22
  34.8 18.9 %all-to-all-done.2 = bf16[256,4,1024]{2,0,1:T(8,128)(2,1)S(1)} async-done(((bf16[256,4,1024]{2,0,1:T(8,128)(2,1)}), bf16[256,4,1024]{2,0,1:T(8,128)(2,1)S(1)}, u32[]{:S(2)}, u32[]{:S(2)}) %all-to-all-start.2) | async-done | bytes 2097184 | tf_op jit(solution)/shard_map/all_to_all | solution.py:33
  53.7 0.6 copy.21
  54.3 3.2 %fusion = (f32[8,8,128]{2,1,0:T(8,128)S(1)}, f32[8,384,128,8]{2,1,3,0:T(8,128)S(1)}) fusion(pred[8,128,384]{1,2,0:T(8,128)(4,1)S(1)} %compare_and_fusion, bf16[8,128,8,128]{3,2,1,0:T(8,128)(2,1)S(1)} %bitcast.92, bf16[8,128,1,128]{3,1,0,2:T(8,128)(2,1)S(1)} %bitcast.96, bf16[8,128,1,128]{3,1,0,2:T(8,128)(2,1)} %bitcast.102, ...), kind=kOutput, calls=%fused_computation.2 | convolution fusion | flops 817094656 | bytes 15892480 | tf_op jit(solution)/shard_map/ctkgd,cskd->ckgts/dot_general | solution.py:69
  57.5 0.0 copy-start.1
  57.5 3.5 %fusion.1 = f32[8,8,128]{2,1,0:T(8,128)S(1)} fusion(f32[8,384,128,8]{2,1,3,0:T(8,128)S(1)} %get-tuple-element.18, f32[8,8,128]{2,1,0:T(8,128)S(1)} %get-tuple-element.17, pred[8,128,384]{1,2,0:T(8,128)(4,1)S(1)} %compare_and_fusion), kind=kLoop, calls=%fused_computation.3 | loop fusion | flops 15720448 | bytes 13041664 | tf_op jit(solution)/shard_map/reduce_sum | solution.py:75
  61.0 0.0 copy-done.1
  61.0 4.7 %fusion.11 = bf16[8,128,1,8,128]{4,1,3,0,2:T(8,128)(2,1)S(1)} fusion(f32[8,8,128]{2,1,0:T(8,128)S(1)} %fusion.1, f32[8,384,128,8]{2,1,3,0:T(8,128)S(1)} %get-tuple-element.18, f32[8,8,128]{2,1,0:T(8,128)S(1)} %get-tuple-element.17, pred[8,128,384]{1,2,0:T(8,128)(4,1)S(1)} %compare_and_fusion, bf16[8,128,1,128]{3,1,0,2:T(8,128)(2,1)S(1)} %bitcast.99, ...), kind=kOutput, calls=%fused_computation.15 | convolution fusion | flops 825491456 | bytes 15925248 | tf_op jit(solution)/shard_map/ckgts,cskd->ckgtd/dot_general | solution.py:76
  65.8 1.4 copy.14
  67.2 14.3 %convolution_convert_fusion = bf16[1024,4096]{1,0:T(8,128)(2,1)} fusion(bf16[1024,4096]{1,0:T(8,128)(2,1)} %param.9, bf16[128,8,8,128]{3,2,1,0:T(8,128)(2,1)S(1)} %bitcast.93), kind=kOutput, calls=%fused_computation.5 | convolution fusion | flops 8594128896 | bytes 18874368 | tf_op jit(solution)/shard_map/dot_general | solution.py:85
  81.4 0.0 reduce-scatter.2.cloned.1.call-update
  81.4 86.7 %reduce-scatter.2.cloned.1.call-done = bf16[256,4096]{1,0:T(8,128)(2,1)} async-done(((bf16[1024,4096]{1,0:T(8,128)(2,1)}), bf16[256,4096]{1,0:T(8,128)(2,1)}) %reduce-scatter.2.cloned.1.call-update) | async-done | bytes 2097168 | tf_op jit(solution)/shard_map/reduce_scatter | solution.py:84
  (8 shorter events, 0.1 us)
Async XLA Ops:
  6.5 1.0 copy-start
  6.5 24.7 %copy-start.2 = (s32[8192]{0:T(1024)S(1)}, s32[8192]{0:T(1024)}, u32[]{:S(2)}) copy-start(s32[8192]{0:T(1024)} %param.8) | copy-start | bytes 98308
  8.2 10.6 %all-to-all-start = ((bf16[256,4,128]{2,0,1:T(8,128)(2,1)}), bf16[256,4,128]{2,0,1:T(8,128)(2,1)S(1)}, u32[]{:S(2)}, u32[]{:S(2)}) async-start(bf16[256,4,128]{2,0,1:T(8,128)(2,1)} %copy_bitcast_fusion.2), calls=%async_computation | async-start | bytes 524288 | tf_op jit(solution)/shard_map/all_to_all | solution.py:34
  18.8 8.8 %all-to-all-start.1 = ((bf16[256,4,128]{2,0,1:T(8,128)(2,1)}), bf16[256,4,128]{2,0,1:T(8,128)(2,1)S(1)}, u32[]{:S(2)}, u32[]{:S(2)}) async-start(bf16[256,4,128]{2,0,1:T(8,128)(2,1)} %copy_bitcast_fusion.1), calls=%async_computation.1 | async-start | bytes 524288 | tf_op jit(solution)/shard_map/all_to_all | solution.py:35
  27.6 26.2 %all-to-all-start.2 = ((bf16[256,4,1024]{2,0,1:T(8,128)(2,1)}), bf16[256,4,1024]{2,0,1:T(8,128)(2,1)S(1)}, u32[]{:S(2)}, u32[]{:S(2)}) async-start(bf16[256,4,1024]{2,0,1:T(8,128)(2,1)} %bitcast.89), calls=%async_computation.2 | async-start | bytes 4194304 | tf_op jit(solution)/shard_map/all_to_all | solution.py:33
  31.2 137.0 %reduce-scatter.2.cloned.1.call-start = ((), (), s32[]{:S(2)}) async-start(), calls=%async_computation.4 | async-start | bytes 10485760 | tf_op jit(solution)/shard_map/reduce_scatter | solution.py:84
  31.4 2.5 %collective-permute-start = (bf16[2,256,128]{2,1,0:T(8,128)(2,1)S(1)}, bf16[2,256,128]{2,1,0:T(8,128)(2,1)S(1)}, u32[]{:S(2)}, u32[]{:S(2)}) collective-permute-start(bf16[2,256,128]{2,1,0:T(8,128)(2,1)S(1)} %pad_maximum_fusion.2), channel_id=1, source_target_pairs={{0,4},{4,8},{8,12},{12,16},{16,20},{20,24},{24,28},{1,5},{5,9},{9,... | collective-permute-start | bytes 393224 | tf_op jit(solution)/shard_map/ppermute | solution.py:14
  57.5 3.5 %copy-start.1 = (bf16[1024,128]{1,0:T(8,128)(2,1)S(1)}, bf16[1024,128]{1,0:T(8,128)(2,1)}, u32[]{:S(2)}) copy-start(bf16[1024,128]{1,0:T(8,128)(2,1)} %get-tuple-element.6) | copy-start | bytes 786436
Sparse Core Ops, SparseCore 0:
  81.6 86.5 reduce-scatter.1
where the time goes:
time: 176 us; the launch traced here: 175 us
  waiting for transfers between devices  112 us (64%)
  matrix products  22.2 us (13%)
  starting transfers between devices  13.5 us (8%)
  between operations  13.5 us (8%)
  local copies, waits for them, and re-layouts  8.66 us (5%)
  other arithmetic  5.6 us (3%)
    reduce_scatter x1, waiting for transfers between devices, shards(): lax.psum_scatter(jnp.dot(attended, out_weight, preferred_element_type=jnp...  86.7 us
    all_to_all x1, waiting for transfers between devices, shards(): lax.all_to_all(queries, 'tp', split_axis=1, concat_axis=0, tiled=True)  18.9 us
    dot_general x1, matrix products, shards(): jnp.dot(attended, out_weight, preferred_element_type=jnp.float32)  14.3 us
    all_to_all x1, starting transfers between devices, shards(): lax.all_to_all(keys_wide, 'tp', split_axis=1, concat_axis=0, tiled=True)  5.19 us
    dot_general x1, matrix products, shards(): jnp.einsum('ckgts,cskd->ckgtd', weights.astype(jnp.bfloat16), value_win,...  4.75 us
    all_to_all x1, waiting for transfers between devices, shards(): lax.all_to_all(keys_wide, 'tp', split_axis=1, concat_axis=0, tiled=True)  3.67 us
    all_to_all x1, starting transfers between devices, shards(): lax.all_to_all(queries, 'tp', split_axis=1, concat_axis=0, tiled=True)  3.61 us
  transfers between devices with their start and end apart: 5, of which 4 were waited for; matrix products, arithmetic and copies ran while one was open for 4% of the time, Pallas kernels for 0%

commit v1 on v0

--- a/solution.py
+++ b/solution.py
@@ -1,11 +1,16 @@
+import functools
+
 import jax
 import jax.numpy as jnp
 from jax import lax
+from jax.experimental import pallas as pl
+from jax.experimental.pallas import tpu as pltpu
 from jax.sharding import PartitionSpec as P
 
 KVH = 4
 HD = 128
 DOC = 256
+TILE = DOC // 2
 
 
 def from_behind(value, axis, steps):
@@ -22,7 +27,7 @@
     return widened.reshape(rows, KVH * copies * HD)
 
 
-def shards(queries, keys, values, segments, out_weight):
+def general_shards(queries, keys, values, segments, out_weight):
     tp_count = lax.axis_size("tp")
     copies = max(tp_count // KVH, 1)
     tile_rows = DOC // 2
@@ -89,6 +94,317 @@
     )
 
 
+DIAG, XN, YN, OWN = 0, 1, 2, 3
+FIRST_CHUNKS = 2
+LAST_CHUNKS = 4
+
+
+def kernel(
+    n_seq,
+    q_hbm,
+    k_hbm,
+    v_hbm,
+    seg_ref,
+    w_hbm,
+    out_ref,
+    qbuf,
+    kext,
+    vext,
+    w_ref,
+    att,
+    bias,
+    part,
+    rx1,
+    ry1,
+    rx2,
+    ry2,
+    local_sem,
+    in_send,
+    in_recv,
+    halo_send,
+    halo_recv,
+    one_send,
+    one_recv,
+    two_send,
+    two_recv,
+):
+    rows, width = qbuf.shape[1], qbuf.shape[2]
+    heads = width // HD
+    n_out = w_ref.shape[1]
+    half = n_out // 2
+    s = lax.axis_index("seq")
+    me = lax.axis_index("tp")
+    x = me % 2
+    y = me // 2
+    ids = (3 - me, y * 2 + 1 - x, (1 - y) * 2 + x, me)
+    closing = me == 3
+    sends_on = jnp.logical_and(closing, s < n_seq - 1)
+
+    def cols(owner, size):
+        return pl.ds(pl.multiple_of(owner * size, 128), size)
+
+    def block(owner):
+        return pl.ds(pl.multiple_of((owner + 1) * rows, rows), rows)
+
+    locals_ = [
+        pltpu.make_async_copy(k_hbm.at[:, cols(me, HD)], kext.at[block(me)], local_sem.at[0]),
+        pltpu.make_async_copy(v_hbm.at[:, cols(me, HD)], vext.at[block(me)], local_sem.at[1]),
+        pltpu.make_async_copy(q_hbm.at[:, cols(me, width)], qbuf.at[OWN], local_sem.at[2]),
+        pltpu.make_async_copy(w_hbm, w_ref, local_sem.at[3]),
+    ]
+    for copy in locals_:
+        copy.start()
+
+    barrier = pltpu.get_barrier_semaphore()
+    for kind in (DIAG, XN, YN):
+        pl.semaphore_signal(barrier, inc=1, device_id={"tp": ids[kind]})
+
+    @pl.when(s > 0)
+    def _():
+        pl.semaphore_signal(barrier, inc=1, device_id={"seq": s - 1, "tp": 3})
+
+    @pl.when(sends_on)
+    def _():
+        for d in range(4):
+            pl.semaphore_signal(barrier, inc=1, device_id={"seq": s + 1, "tp": d})
+
+    behind = jnp.where(s > 0, 1, 0)
+    ahead = jnp.where(sends_on, 4, 0)
+    pl.semaphore_wait(barrier, 3 + behind + ahead)
+
+    def inward(kind, which):
+        src, dst, size = (
+            (k_hbm, kext.at[block(me)], HD),
+            (v_hbm, vext.at[block(me)], HD),
+            (q_hbm, qbuf.at[kind], width),
+        )[which]
+        return pltpu.make_async_remote_copy(
+            src_ref=src.at[:, cols(ids[kind], size)],
+            dst_ref=dst,
+            send_sem=in_send.at[which, kind],
+            recv_sem=in_recv.at[which, kind],
+            device_id={"tp": ids[kind]},
+        )
+
+    def halo(d, which):
+        return pltpu.make_async_remote_copy(
+            src_ref=(k_hbm, v_hbm)[which].at[:, pl.ds(d * HD, HD)],
+            dst_ref=(kext, vext)[which].at[pl.ds(0, rows)],
+            send_sem=halo_send.at[which, d],
+            recv_sem=halo_recv.at[which],
+            device_id={"seq": lax.rem(s + 1, n_seq), "tp": d},
+        )
+
+    arrivals = {(k, w): inward(k, w) for w in range(3) for k in (DIAG, XN, YN)}
+    for kind in (DIAG, XN, YN):
+        arrivals[kind, 0].start()
+        arrivals[kind, 1].start()
+
+    @pl.when(sends_on)
+    def _():
+        for d in range(4):
+            halo(d, 0).start()
+            halo(d, 1).start()
+
+    for kind in (DIAG, XN, YN):
+        arrivals[kind, 2].start()
+
+    @pl.when(s == 0)
+    def _():
+        kext[0:rows] = jnp.zeros((rows, HD), kext.dtype)
+        vext[0:rows] = jnp.zeros((rows, HD), vext.dtype)
+
+    for copy in locals_:
+        copy.wait()
+    for kind in (DIAG, XN, YN):
+        arrivals[kind, 0].wait_recv()
+        arrivals[kind, 1].wait_recv()
+
+    @pl.when(s > 0)
+    def _():
+        halo(0, 0).wait_recv()
+        halo(0, 1).wait_recv()
+
+    tiles = rows // TILE
+    causal_q = lax.broadcasted_iota(jnp.int32, (TILE, TILE), 0)
+    causal_k = lax.broadcasted_iota(jnp.int32, (TILE, TILE), 1)
+
+    def attend(kind):
+        owner = ids[kind]
+
+        @pl.loop(0, tiles)
+        def _(t):
+            row = (s * 4 + owner) * tiles + t
+
+            def seg_row(at):
+                got = seg_ref[pl.ds(jnp.maximum(at, 0), 1), :]
+                return jnp.broadcast_to(jnp.where(at >= 0, got, -1), (TILE, TILE))
+
+            mine = seg_row(row)
+            down = jnp.transpose(mine)
+            low = jnp.float32(-1e30)
+            zero = jnp.float32(0.0)
+            bias[:, 0:TILE] = jnp.where(seg_row(row - 2) == down, zero, low)
+            bias[:, TILE : 2 * TILE] = jnp.where(seg_row(row - 1) == down, zero, low)
+            bias[:, 2 * TILE : 3 * TILE] = jnp.where(
+                jnp.logical_and(mine == down, causal_k <= causal_q), zero, low
+            )
+            start = pl.multiple_of(owner * rows + t * TILE, TILE)
+            here = pl.ds(pl.multiple_of(t * TILE, TILE), TILE)
+            key_win = kext[pl.ds(start, 3 * TILE), :]
+            value_win = vext[pl.ds(start, 3 * TILE), :]
+            for h in range(heads):
+                span = slice(h * HD, (h + 1) * HD)
+                scores = lax.dot_general(
+                    qbuf[kind, here, span],
+                    key_win,
+                    (((1,), (1,)), ((), ())),
+                    preferred_element_type=jnp.float32,
+                )
+                scores = scores * (HD**-0.5) + bias[...]
+                weights = jnp.exp(scores - jnp.max(scores, axis=-1, keepdims=True))
+                denom = jnp.sum(weights, axis=-1, keepdims=True)
+                total = jnp.dot(
+                    weights.astype(jnp.bfloat16), value_win, preferred_element_type=jnp.float32
+                )
+                att[here, span] = (total / denom).astype(jnp.bfloat16)
+
+    step = 512
+
+    def project(kind):
+        @pl.loop(0, n_out // step)
+        def _(j):
+            at = pl.ds(pl.multiple_of(j * step, step), step)
+            part[kind, :, at] = jnp.dot(
+                att[...], w_ref[:, at], preferred_element_type=jnp.float32
+            ).astype(jnp.bfloat16)
+
+    lo, hi = slice(0, half), slice(half, n_out)
+    first_rows = rows // FIRST_CHUNKS
+    last_rows = rows // LAST_CHUNKS
+
+    def one(axis, slot, c):
+        at = pl.ds(c * first_rows, first_rows)
+        kind = DIAG if slot == 0 else (XN, YN)[axis]
+        return pltpu.make_async_remote_copy(
+            src_ref=part.at[kind, at, pl.ds((0, half)[axis], half)],
+            dst_ref=(rx1, ry1)[axis].at[slot, at],
+            send_sem=one_send.at[axis, slot, c],
+            recv_sem=one_recv.at[axis, slot, c],
+            device_id={"tp": ids[(XN, YN)[axis]]},
+        )
+
+    def two(axis, c):
+        at = pl.ds(c * last_rows, last_rows)
+        return pltpu.make_async_remote_copy(
+            src_ref=part.at[(XN, YN)[axis], at, pl.ds((half, 0)[axis], half)],
+            dst_ref=(rx2, ry2)[axis].at[at],
+            send_sem=two_send.at[axis, c],
+            recv_sem=two_recv.at[axis, c],
+            device_id={"tp": ids[(XN, YN)[axis]]},
+        )
+
+    for kind in (DIAG, XN, YN, OWN):
+        if kind != OWN:
+            arrivals[kind, 2].wait_recv()
+        attend(kind)
+        project(kind)
+        for c in range(FIRST_CHUNKS):
+            if kind in (DIAG, XN):
+                one(0, 0 if kind == DIAG else 1, c).start()
+            if kind in (DIAG, YN):
+                one(1, 0 if kind == DIAG else 1, c).start()
+
+    f32 = jnp.float32
+    per = LAST_CHUNKS // FIRST_CHUNKS
+    for c in range(FIRST_CHUNKS):
+        one(0, 0, c).wait_recv()
+        for i in range(c * per, (c + 1) * per):
+            at = slice(i * last_rows, (i + 1) * last_rows)
+            part[YN, at, lo] = (part[YN, at, lo].astype(f32) + rx1[0, at].astype(f32)).astype(
+                jnp.bfloat16
+            )
+            two(1, i).start()
+        one(1, 0, c).wait_recv()
+        for i in range(c * per, (c + 1) * per):
+            at = slice(i * last_rows, (i + 1) * last_rows)
+            part[XN, at, hi] = (part[XN, at, hi].astype(f32) + ry1[0, at].astype(f32)).astype(
+                jnp.bfloat16
+            )
+            two(0, i).start()
+    for c in range(FIRST_CHUNKS):
+        one(0, 1, c).wait_recv()
+        one(1, 1, c).wait_recv()
+    for i in range(LAST_CHUNKS):
+        at = slice(i * last_rows, (i + 1) * last_rows)
+        two(1, i).wait_recv()
+        out_ref[at, lo] = (
+            part[OWN, at, lo].astype(f32) + rx1[1, at].astype(f32) + ry2[at].astype(f32)
+        ).astype(jnp.bfloat16)
+        two(0, i).wait_recv()
+        out_ref[at, hi] = (
+            part[OWN, at, hi].astype(f32) + ry1[1, at].astype(f32) + rx2[at].astype(f32)
+        ).astype(jnp.bfloat16)
+
+    for copy in arrivals.values():
+        copy.wait_send()
+
+    @pl.when(sends_on)
+    def _():
+        for d in range(4):
+            halo(d, 0).wait_send()
+            halo(d, 1).wait_send()
+
+    for axis in range(2):
+        for c in range(FIRST_CHUNKS):
+            one(axis, 0, c).wait_send()
+            one(axis, 1, c).wait_send()
+        for c in range(LAST_CHUNKS):
+            two(axis, c).wait_send()
+
+
+def square_shards(n_seq, queries, keys, values, segments, out_weight):
+    rows, n_q = queries.shape
+    width = n_q // 4
+    depth, n_out = out_weight.shape
+    half = n_out // 2
+    bf16 = jnp.bfloat16
+    any_ = pl.BlockSpec(memory_space=pl.ANY)
+    vmem = pl.BlockSpec(memory_space=pltpu.VMEM)
+    dma = pltpu.SemaphoreType.DMA
+    return pl.pallas_call(
+        functools.partial(kernel, n_seq),
+        out_shape=jax.ShapeDtypeStruct((rows, n_out), bf16),
+        in_specs=[any_, any_, any_, vmem, any_],
+        out_specs=vmem,
+        scratch_shapes=[
+            pltpu.VMEM((4, rows, width), bf16),
+            pltpu.VMEM((5 * rows, HD), bf16),
+            pltpu.VMEM((5 * rows, HD), bf16),
+            pltpu.VMEM((depth, n_out), bf16),
+            pltpu.VMEM((rows, width), bf16),
+            pltpu.VMEM((TILE, 3 * TILE), jnp.float32),
+            pltpu.VMEM((4, rows, n_out), bf16),
+            pltpu.VMEM((2, rows, half), bf16),
+            pltpu.VMEM((2, rows, half), bf16),
+            pltpu.VMEM((rows, half), bf16),
+            pltpu.VMEM((rows, half), bf16),
+            dma((4,)),
+            dma((3, 3)),
+            dma((3, 3)),
+            dma((2, 4)),
+            dma((2,)),
+            dma((2, 2, FIRST_CHUNKS)),
+            dma((2, 2, FIRST_CHUNKS)),
+            dma((2, LAST_CHUNKS)),
+            dma((2, LAST_CHUNKS)),
+        ],
+        compiler_params=pltpu.CompilerParams(
+            collective_id=0, has_side_effects=True, vmem_limit_bytes=48 * 1024 * 1024
+        ),
+    )(queries, keys, values, segments.reshape(-1, TILE), out_weight)
+
+
 def solution(mesh):
     placed = (
         P(("seq", "tp"), None),
@@ -97,6 +413,14 @@
         P(),
         P("tp", None),
     )
+    n_seq, n_tp = mesh.shape["seq"], mesh.shape["tp"]
+
+    def shards(queries, keys, values, segments, out_weight):
+        one_head_each = keys.shape[1] == n_tp * HD
+        if n_tp == 4 and one_head_each and queries.shape[0] == DOC:
+            return square_shards(n_seq, queries, keys, values, segments, out_weight)
+        return general_shards(queries, keys, values, segments, out_weight)
+
     return jax.shard_map(
         shards, mesh=mesh, in_specs=placed, out_specs=P(("seq", "tp"), None), check_vma=False
     )

time: 176 us -> 111 us (0.63)
  the two profiles are of different devices: /device:TPU:0 before, /device:TPU:12 now
where the time goes in v1:
time: 111 us
  Pallas kernels  106 us (95%)
  local copies, waits for them, and re-layouts  5.57 us (5%)
    pallas_call x1, Pallas kernels, square_shards(): pl.pallas_call(functools.partial(kernel, n_seq), out_shape=jax.ShapeDtype...  106 us
    unnamed x9, local copies, waits for them, and re-layouts  5.57 us

profile of v1, /device:TPU:12, one launch (start us, length us, event | category | flops | bytes accessed | tf_op | source)
XLA Modules:
  0.0 111.1 jit_solution(3688580643283313131)
XLA Ops:
  0.0 0.0 copy-start
  0.0 1.6 %copy-done = bf16[256,4096]{1,0:T(8,128)(2,1)S(1)} copy-done((bf16[256,4096]{1,0:T(8,128)(2,1)S(1)}, bf16[256,4096]{1,0:T(8,128)(2,1)}, u32[]{:S(2)}) %copy-start) | copy-done | bytes 2097176
  1.6 0.0 copy-start.1
  1.6 0.9 copy-done.1
  2.5 0.0 copy-start.2
  2.5 0.9 copy-done.2
  3.5 0.0 copy-start.3
  3.5 0.8 copy-done.3
  4.3 105.6 %shard_map.55 = bf16[256,4096]{1,0:T(8,128)(2,1)S(1)} custom-call(bf16[256,4096]{1,0:T(8,128)(2,1)S(1)} %copy-done, bf16[256,512]{1,0:T(8,128)(2,1)S(1)} %copy-done.1, bf16[256,512]{1,0:T(8,128)(2,1)S(1)} %copy-done.2, s32[64,128]{1,0:T(8,128)S(1)} %bitcast.1, bf16[1024,4096]{1,0:T(8,128)(2,1)} %w_hbm.1), custom_call_target="tpu_custom_call" | custom-call | tf_op jit(solution)/shard_map/pallas_call | solution.py:375
  109.8 1.3 %copy.7 = bf16[256,4096]{1,0:T(8,128)(2,1)} copy(bf16[256,4096]{1,0:T(8,128)(2,1)S(1)} %shard_map.55) | data formatting | bytes 4194304
Async XLA Ops:
  0.0 1.6 %copy-start = (bf16[256,4096]{1,0:T(8,128)(2,1)S(1)}, bf16[256,4096]{1,0:T(8,128)(2,1)}, u32[]{:S(2)}) copy-start(bf16[256,4096]{1,0:T(8,128)(2,1)} %q_hbm.1) | copy-start | bytes 6291460
  1.6 0.9 copy-start.1
  2.5 0.9 copy-start.2
  3.5 0.8 copy-start.3

commit v2 on v0

--- a/solution.py
+++ b/solution.py
@@ -1,11 +1,16 @@
+import functools
+
 import jax
 import jax.numpy as jnp
 from jax import lax
+from jax.experimental import pallas as pl
+from jax.experimental.pallas import tpu as pltpu
 from jax.sharding import PartitionSpec as P
 
 KVH = 4
 HD = 128
 DOC = 256
+TILE = DOC // 2
 
 
 def from_behind(value, axis, steps):
@@ -22,7 +27,7 @@
     return widened.reshape(rows, KVH * copies * HD)
 
 
-def shards(queries, keys, values, segments, out_weight):
+def general_shards(queries, keys, values, segments, out_weight):
     tp_count = lax.axis_size("tp")
     copies = max(tp_count // KVH, 1)
     tile_rows = DOC // 2
@@ -89,6 +94,340 @@
     )
 
 
+PAIRS = 8
+
+
+def kernel(
+    n_seq,
+    q_hbm,
+    k_hbm,
+    v_hbm,
+    seg_ref,
+    w_hbm,
+    out_ref,
+    qbuf,
+    kwin,
+    vwin,
+    w_ref,
+    w_side,
+    att,
+    bias,
+    part,
+    own,
+    arrived,
+    local_sem,
+    in_send,
+    in_recv,
+    before_send,
+    before_recv,
+    w_send,
+    w_recv,
+    out_send,
+    out_recv,
+):
+    rows, width = qbuf.shape[1], qbuf.shape[2]
+    pair_width = kwin.shape[2]
+    group = width // pair_width
+    depth, n_out = w_ref.shape
+    pair_cols = n_out // PAIRS
+    chunk = pair_cols // 2
+    half = depth // 2
+    s = lax.axis_index("seq")
+    me = lax.axis_index("tp")
+    x = me % 2
+    y = me // 2
+    xn = y * 2 + 1 - x
+    yn = (1 - y) * 2 + x
+    core = s % 2
+    parity = (s // 2) % 2
+    peer = s + 1 - 2 * core
+    plane = s + 2 - 4 * parity
+    blocks = (me, yn)
+    f32, bf16 = jnp.float32, jnp.bfloat16
+
+    def cols(index, size):
+        return pl.ds(pl.multiple_of(index * size, size), size)
+
+    late = pl.ds(rows, rows)
+    early = pl.ds(0, rows)
+    locals_ = [
+        pltpu.make_async_copy(k_hbm.at[:, cols(y, pair_width)], kwin.at[0, late], local_sem.at[0]),
+        pltpu.make_async_copy(v_hbm.at[:, cols(y, pair_width)], vwin.at[0, late], local_sem.at[1]),
+        pltpu.make_async_copy(q_hbm.at[:, cols(y, width)], qbuf.at[0], local_sem.at[2]),
+        pltpu.make_async_copy(w_hbm, w_ref, local_sem.at[3]),
+    ]
+    for copy in locals_:
+        copy.start()
+
+    barrier = pltpu.get_barrier_semaphore()
+    for target in ({"tp": xn}, {"tp": yn}, {"seq": peer}, {"seq": plane}):
+        pl.semaphore_signal(barrier, inc=1, device_id=target)
+    to_next = jnp.logical_and(x == 1, s < n_seq - 1)
+    from_last = jnp.logical_and(x == 0, s > 0)
+
+    @pl.when(to_next)
+    def _():
+        pl.semaphore_signal(barrier, inc=1, device_id={"seq": s + 1, "tp": xn})
+
+    @pl.when(from_last)
+    def _():
+        pl.semaphore_signal(barrier, inc=1, device_id={"seq": s - 1, "tp": xn})
+
+    pl.semaphore_wait(barrier, 4 + jnp.where(to_next, 1, 0) + jnp.where(from_last, 1, 0))
+
+    def across(which):
+        src, dst, size = (
+            (k_hbm, kwin.at[1, late], pair_width),
+            (v_hbm, vwin.at[1, late], pair_width),
+        )[which]
+        return pltpu.make_async_remote_copy(
+            src_ref=src.at[:, cols(1 - y, size)],
+            dst_ref=dst,
+            send_sem=in_send.at[which],
+            recv_sem=in_recv.at[which],
+            device_id={"tp": yn},
+        )
+
+    def across_q(t):
+        at = pl.ds(t * TILE, TILE)
+        return pltpu.make_async_remote_copy(
+            src_ref=q_hbm.at[at, cols(1 - y, width)],
+            dst_ref=qbuf.at[1, at],
+            send_sem=in_send.at[2 + t],
+            recv_sem=in_recv.at[2 + t],
+            device_id={"tp": yn},
+        )
+
+    def before(j, which, hop):
+        win = (kwin, vwin)[which]
+        src = (k_hbm, v_hbm)[which].at[:, cols(y, pair_width)] if j == 0 else win.at[1, late]
+        slot = j + x * (1 - 2 * j)
+        return pltpu.make_async_remote_copy(
+            src_ref=src,
+            dst_ref=win.at[slot, early],
+            send_sem=before_send.at[which, j],
+            recv_sem=before_recv.at[which, slot],
+            device_id={"seq": lax.rem(s + hop, n_seq), "tp": xn},
+        )
+
+    def send_before(j):
+        @pl.when(blocks[j] != 3)
+        def _():
+            before(j, 0, 0).start()
+            before(j, 1, 0).start()
+
+        @pl.when(jnp.logical_and(blocks[j] == 3, s < n_seq - 1))
+        def _():
+            before(j, 0, 1).start()
+            before(j, 1, 1).start()
+
+    def sent_before(j):
+        @pl.when(jnp.logical_or(blocks[j] != 3, s < n_seq - 1))
+        def _():
+            before(j, 0, 0).wait_send()
+            before(j, 1, 0).wait_send()
+
+    def wait_before(j):
+        @pl.when(jnp.logical_or(blocks[j] != 0, s > 0))
+        def _():
+            for which, win in enumerate((kwin, vwin)):
+                pltpu.make_async_remote_copy(
+                    src_ref=win.at[j, early],
+                    dst_ref=win.at[j, early],
+                    send_sem=before_send.at[which, j],
+                    recv_sem=before_recv.at[which, j],
+                    device_id={"tp": xn},
+                ).wait_recv()
+
+    mine = pl.ds(pl.multiple_of(core * half, half), half)
+
+    def weight(i, stage):
+        which = 1 - parity if stage == 3 else parity
+        at = cols(2 * i + which, chunk)
+        return pltpu.make_async_remote_copy(
+            src_ref=(w_hbm if stage == 0 else w_side).at[mine, at],
+            dst_ref=w_side.at[mine, at],
+            send_sem=w_send.at[stage, i],
+            recv_sem=w_recv.at[stage, i],
+            device_id=({"tp": xn}, {"seq": plane}, {"seq": peer}, {"seq": peer})[stage],
+        )
+
+    def relay_direct(i):
+        weight(i, 0).wait_recv()
+        weight(i, 1).start()
+        weight(i, 2).start()
+
+    def relay_plane(i):
+        weight(i, 1).wait_recv()
+        weight(i, 3).start()
+
+    across(0).start()
+    across(1).start()
+    tiles = rows // TILE
+    for t in range(tiles):
+        across_q(t).start()
+    send_before(0)
+    weight(0, 0).start()
+
+    for j in range(2):
+
+        @pl.when(jnp.logical_and(blocks[j] == 0, s == 0))
+        def _():
+            kwin[j, 0:rows] = jnp.zeros((rows, pair_width), bf16)
+            vwin[j, 0:rows] = jnp.zeros((rows, pair_width), bf16)
+
+    across(0).wait_recv()
+    across(1).wait_recv()
+    send_before(1)
+    for i in range(1, PAIRS):
+        weight(i, 0).start()
+    for copy in locals_:
+        copy.wait()
+
+    causal_q = lax.broadcasted_iota(jnp.int32, (TILE, TILE), 0)
+    causal_k = lax.broadcasted_iota(jnp.int32, (TILE, TILE), 1)
+
+    def attend(j, t):
+        row = (s * 4 + blocks[j]) * tiles + t
+
+        def seg_row(at):
+            got = seg_ref[pl.ds(jnp.maximum(at, 0), 1), :]
+            return jnp.broadcast_to(jnp.where(at >= 0, got, -1), (TILE, TILE))
+
+        current = seg_row(row)
+        down = jnp.transpose(current)
+        low, zero = f32(-1e30), f32(0.0)
+        bias[:, 0:TILE] = jnp.where(seg_row(row - 2) == down, zero, low)
+        bias[:, TILE : 2 * TILE] = jnp.where(seg_row(row - 1) == down, zero, low)
+        bias[:, 2 * TILE : 3 * TILE] = jnp.where(
+            jnp.logical_and(current == down, causal_k <= causal_q), zero, low
+        )
+        here = pl.ds(pl.multiple_of(t * TILE, TILE), TILE)
+        window = pl.ds(pl.multiple_of(t * TILE, TILE), 3 * TILE)
+        for h in range(width // HD):
+            span = slice(h * HD, (h + 1) * HD)
+            kv = slice(h // group * HD, (h // group + 1) * HD)
+            scores = lax.dot_general(
+                qbuf[j, here, span],
+                kwin[j, window, kv],
+                (((1,), (1,)), ((), ())),
+                preferred_element_type=f32,
+            )
+            scores = scores * (HD**-0.5) + bias[...]
+            weights = jnp.exp(scores - jnp.max(scores, axis=-1, keepdims=True))
+            denom = jnp.sum(weights, axis=-1, keepdims=True)
+            total = jnp.dot(weights.astype(bf16), vwin[j, window, kv], preferred_element_type=f32)
+            att[j, here, span] = (total / denom).astype(bf16)
+
+    wait_before(0)
+
+    @pl.loop(0, tiles)
+    def _(t):
+        attend(0, t)
+
+    relay_direct(0)
+    wait_before(1)
+    across_q(0).wait_recv()
+    attend(1, 0)
+    relay_direct(1)
+    relay_plane(0)
+    for t in range(1, tiles):
+        across_q(t).wait_recv()
+        attend(1, t)
+
+    def product(j, at):
+        return jnp.dot(
+            att[j, :, cols(x, depth)], w_ref[:, at], preferred_element_type=f32
+        ) + jnp.dot(att[j, :, cols(1 - x, depth)], w_side[:, at], preferred_element_type=f32)
+
+    def outward(i):
+        at = cols(i, pair_cols)
+        return pltpu.make_async_remote_copy(
+            src_ref=part.at[:, at],
+            dst_ref=arrived.at[:, at],
+            send_sem=out_send.at[i],
+            recv_sem=out_recv.at[i],
+            device_id={"tp": yn},
+        )
+
+    @pl.loop(0, PAIRS)
+    def _(i):
+        @pl.when(i + 2 < PAIRS)
+        def _():
+            relay_direct(i + 2)
+
+        @pl.when(i + 1 < PAIRS)
+        def _():
+            relay_plane(i + 1)
+
+        weight(i, 2).wait_recv()
+        weight(i, 3).wait_recv()
+        at = cols(i, pair_cols)
+        part[:, at] = product(1, at).astype(bf16)
+        outward(i).start()
+        own[:, at] = product(0, at)
+
+    @pl.loop(0, PAIRS)
+    def _(i):
+        at = cols(i, pair_cols)
+        outward(i).wait_recv()
+        out_ref[:, at] = (own[:, at] + arrived[:, at].astype(f32)).astype(bf16)
+
+    across(0).wait_send()
+    across(1).wait_send()
+    for t in range(tiles):
+        across_q(t).wait_send()
+    sent_before(0)
+    sent_before(1)
+
+    @pl.loop(0, PAIRS)
+    def _(i):
+        for stage in range(4):
+            weight(i, stage).wait_send()
+        outward(i).wait_send()
+
+
+def square_shards(n_seq, queries, keys, values, segments, out_weight):
+    rows, n_q = queries.shape
+    width = n_q // 2
+    pair_width = keys.shape[1] // 2
+    depth, n_out = out_weight.shape
+    bf16 = jnp.bfloat16
+    hbm = pl.BlockSpec(memory_space=pltpu.HBM)
+    vmem = pl.BlockSpec(memory_space=pltpu.VMEM)
+    dma = pltpu.SemaphoreType.DMA
+    return pl.pallas_call(
+        functools.partial(kernel, n_seq),
+        out_shape=jax.ShapeDtypeStruct((rows, n_out), bf16),
+        in_specs=[hbm, hbm, hbm, vmem, hbm],
+        out_specs=vmem,
+        scratch_shapes=[
+            pltpu.VMEM((2, rows, width), bf16),
+            pltpu.VMEM((2, 2 * rows, pair_width), bf16),
+            pltpu.VMEM((2, 2 * rows, pair_width), bf16),
+            pltpu.VMEM((depth, n_out), bf16),
+            pltpu.VMEM((depth, n_out), bf16),
+            pltpu.VMEM((2, rows, width), bf16),
+            pltpu.VMEM((TILE, 3 * TILE), jnp.float32),
+            pltpu.VMEM((rows, n_out), bf16),
+            pltpu.VMEM((rows, n_out), jnp.float32),
+            pltpu.VMEM((rows, n_out), bf16),
+            dma((4,)),
+            dma((2 + rows // TILE,)),
+            dma((2 + rows // TILE,)),
+            dma((2, 2)),
+            dma((2, 2)),
+            dma((4, PAIRS)),
+            dma((4, PAIRS)),
+            dma((PAIRS,)),
+            dma((PAIRS,)),
+        ],
+        compiler_params=pltpu.CompilerParams(
+            collective_id=0, has_side_effects=True, vmem_limit_bytes=52 * 1024 * 1024
+        ),
+    )(queries, keys, values, segments.reshape(-1, TILE), out_weight)
+
+
 def solution(mesh):
     placed = (
         P(("seq", "tp"), None),
@@ -97,6 +436,15 @@
         P(),
         P("tp", None),
     )
+    n_seq, n_tp = mesh.shape["seq"], mesh.shape["tp"]
+
+    def shards(queries, keys, values, segments, out_weight):
+        one_head_each = keys.shape[1] == n_tp * HD
+        fits = n_tp == 4 and n_seq % 4 == 0 and queries.shape[0] == DOC
+        if fits and one_head_each:
+            return square_shards(n_seq, queries, keys, values, segments, out_weight)
+        return general_shards(queries, keys, values, segments, out_weight)
+
     return jax.shard_map(
         shards, mesh=mesh, in_specs=placed, out_specs=P(("seq", "tp"), None), check_vma=False
     )

time: 176 us -> 101 us (0.57)
  waiting for transfers between devices: 112 us -> 0 us
  Pallas kernels: 0 us -> 95.4 us
  matrix products: 22.2 us -> 0 us
  starting transfers between devices: 13.5 us -> 0 us
  between operations: 13.5 us -> 0.01 us
  other arithmetic: 5.6 us -> 0 us
  local copies, waits for them, and re-layouts: 8.66 us -> 5.79 us
    pallas_call x0 -> x1, Pallas kernels: none -> 95.4 us  [square_shards(): pl.pallas_call(functools.partial(kernel, n_seq), out_shape=jax.ShapeDtype...]
    reduce_scatter x1 -> x0, waiting for transfers between devices: 86.7 us -> none  [shards(): lax.psum_scatter(jnp.dot(attended, out_weight, preferred_element_type=jnp...]
    all_to_all x3 -> x0, waiting for transfers between devices: 24.8 us -> none  [the longest x1 18.9 us: shards(): lax.all_to_all(queries, 'tp', split_axis=1, concat_axis=0, tiled=True)]
    dot_general x3 -> x0, matrix products: 22.2 us -> none  [the longest x1 14.3 us: shards(): jnp.dot(attended, out_weight, preferred_element_type=jnp.float32)]
    all_to_all x3 -> x0, starting transfers between devices: 12.2 us -> none  [the longest x1 5.19 us: shards(): lax.all_to_all(keys_wide, 'tp', split_axis=1, concat_axis=0, tiled=True)]
    all_to_all x3 -> x0, local copies, waits for them, and re-layouts: 5.59 us -> none  [the longest x1 3.14 us: shards(): lax.all_to_all(queries, 'tp', split_axis=1, concat_axis=0, tiled=True)]
    unnamed x7, local copies, waits for them, and re-layouts: 1.57 us -> 5.79 us
    reduce_sum x1 -> x0, other arithmetic: 3.49 us -> none  [shards(): denominator = jnp.sum(weights, axis=-1)]
  transfers between devices with their start and end apart: 5 -> 0, of which waited for: 4 -> 0; matrix products, arithmetic and copies ran while one was open for 4% -> 0% of each run, Pallas kernels for 0% -> 0%
where the time goes in v2:
time: 101 us
  Pallas kernels  95.4 us (94%)
  local copies, waits for them, and re-layouts  5.79 us (6%)
    pallas_call x1, Pallas kernels, square_shards(): pl.pallas_call(functools.partial(kernel, n_seq), out_shape=jax.ShapeDtype...  95.4 us
    unnamed x7, local copies, waits for them, and re-layouts  5.79 us

profile of v2, /device:TPU:0, one launch (start us, length us, event | category | flops | bytes accessed | tf_op | source)
XLA Modules:
  0.0 101.2 jit_solution(12086742978518184437)
XLA Ops:
  0.0 0.0 copy-start
  0.0 0.9 copy-done
  1.0 0.0 copy-start.1
  1.0 0.9 copy-done.1
  1.9 0.0 copy-start.2
  1.9 0.8 copy-done.2
  2.7 95.4 %shard_map.55 = bf16[256,4096]{1,0:T(8,128)(2,1)} custom-call(bf16[256,4096]{1,0:T(8,128)(2,1)} %q_hbm.1, bf16[256,512]{1,0:T(8,128)(2,1)S(1)} %copy-done, bf16[256,512]{1,0:T(8,128)(2,1)S(1)} %copy-done.1, s32[64,128]{1,0:T(8,128)S(1)} %bitcast.1, bf16[1024,4096]{1,0:T(8,128)(2,1)} %w_hbm.1), custom_call_target="tpu_custom_call" | custom-call | tf_op jit(solution)/shard_map/pallas_call | solution.py:399
  98.1 3.1 %copy.7 = bf16[256,4096]{1,0:T(8,128)(2,1)} copy(bf16[256,4096]{1,0:T(8,128)(2,1)} %shard_map.55) | data formatting | bytes 4194304
Async XLA Ops:
  0.0 0.9 copy-start
  1.0 0.9 copy-start.1
  1.9 0.8 copy-start.2

commit v3 on v2

--- a/solution.py
+++ b/solution.py
@@ -334,6 +334,7 @@
     for t in range(1, tiles):
         across_q(t).wait_recv()
         attend(1, t)
+    relay_direct(2)
 
     def product(j, at):
         return jnp.dot(
@@ -352,20 +353,20 @@
 
     @pl.loop(0, PAIRS)
     def _(i):
-        @pl.when(i + 2 < PAIRS)
-        def _():
-            relay_direct(i + 2)
-
-        @pl.when(i + 1 < PAIRS)
-        def _():
-            relay_plane(i + 1)
-
         weight(i, 2).wait_recv()
         weight(i, 3).wait_recv()
         at = cols(i, pair_cols)
         part[:, at] = product(1, at).astype(bf16)
         outward(i).start()
         own[:, at] = product(0, at)
+
+        @pl.when(i + 1 < PAIRS)
+        def _():
+            relay_plane(i + 1)
+
+        @pl.when(i + 3 < PAIRS)
+        def _():
+            relay_direct(i + 3)
 
     @pl.loop(0, PAIRS)
     def _(i):
@@ -423,7 +424,7 @@
             dma((PAIRS,)),
         ],
         compiler_params=pltpu.CompilerParams(
-            collective_id=0, has_side_effects=True, vmem_limit_bytes=52 * 1024 * 1024
+            collective_id=0, has_side_effects=True, vmem_limit_bytes=44 * 1024 * 1024
         ),
     )(queries, keys, values, segments.reshape(-1, TILE), out_weight)
 

time: 101 us -> 98.6 us (0.976)
  Pallas kernels: 95.4 us -> 92.8 us
    pallas_call x1, Pallas kernels: 95.4 us -> 92.8 us  [square_shards(): pl.pallas_call(functools.partial(kernel, n_seq), out_shape=jax.ShapeDtype...]
    unnamed x7 -> x9, local copies, waits for them, and re-layouts: 5.79 us -> 5.57 us
where the time goes in v3:
time: 98.6 us; the launch traced here: 98.3 us
  Pallas kernels  92.8 us (94%)
  local copies, waits for them, and re-layouts  5.57 us (6%)
    pallas_call x1, Pallas kernels, square_shards(): pl.pallas_call(functools.partial(kernel, n_seq), out_shape=jax.ShapeDtype...  92.8 us
    unnamed x9, local copies, waits for them, and re-layouts  5.57 us

profile of v3, /device:TPU:0, one launch (start us, length us, event | category | flops | bytes accessed | tf_op | source)
XLA Modules:
  0.0 98.3 jit_solution(8285370372946755049)
XLA Ops:
  0.0 0.0 copy-start
  0.0 1.6 %copy-done = bf16[256,4096]{1,0:T(8,128)(2,1)S(1)} copy-done((bf16[256,4096]{1,0:T(8,128)(2,1)S(1)}, bf16[256,4096]{1,0:T(8,128)(2,1)}, u32[]{:S(2)}) %copy-start) | copy-done | bytes 2097176
  1.6 0.0 copy-start.1
  1.6 0.9 copy-done.1
  2.5 0.0 copy-start.2
  2.5 0.9 copy-done.2
  3.5 0.0 copy-start.3
  3.5 0.8 copy-done.3
  4.3 92.8 %shard_map.55 = bf16[256,4096]{1,0:T(8,128)(2,1)S(1)} custom-call(bf16[256,4096]{1,0:T(8,128)(2,1)S(1)} %copy-done, bf16[256,512]{1,0:T(8,128)(2,1)S(1)} %copy-done.1, bf16[256,512]{1,0:T(8,128)(2,1)S(1)} %copy-done.2, s32[64,128]{1,0:T(8,128)S(1)} %bitcast.1, bf16[1024,4096]{1,0:T(8,128)(2,1)} %w_hbm.1), custom_call_target="tpu_custom_call" | custom-call | tf_op jit(solution)/shard_map/pallas_call | solution.py:400
  97.0 1.3 %copy.7 = bf16[256,4096]{1,0:T(8,128)(2,1)} copy(bf16[256,4096]{1,0:T(8,128)(2,1)S(1)} %shard_map.55) | data formatting | bytes 4194304
Async XLA Ops:
  0.0 1.6 %copy-start = (bf16[256,4096]{1,0:T(8,128)(2,1)S(1)}, bf16[256,4096]{1,0:T(8,128)(2,1)}, u32[]{:S(2)}) copy-start(bf16[256,4096]{1,0:T(8,128)(2,1)} %q_hbm.1) | copy-start | bytes 6291460
  1.6 0.9 copy-start.1
  2.5 0.9 copy-start.2
  3.5 0.8 copy-start.3

commit v4 on v3

--- a/solution.py
+++ b/solution.py
@@ -188,13 +188,14 @@
             device_id={"tp": yn},
         )
 
-    def across_q(t):
+    def across_q(t, g):
         at = pl.ds(t * TILE, TILE)
+        part_width = width // 2
         return pltpu.make_async_remote_copy(
-            src_ref=q_hbm.at[at, cols(1 - y, width)],
-            dst_ref=qbuf.at[1, at],
-            send_sem=in_send.at[2 + t],
-            recv_sem=in_recv.at[2 + t],
+            src_ref=q_hbm.at[at, cols((1 - y) * 2 + g, part_width)],
+            dst_ref=qbuf.at[1, at, pl.ds(g * part_width, part_width)],
+            send_sem=in_send.at[2 + 2 * t + g],
+            recv_sem=in_recv.at[2 + 2 * t + g],
             device_id={"tp": yn},
         )
 
@@ -265,7 +266,8 @@
     across(1).start()
     tiles = rows // TILE
     for t in range(tiles):
-        across_q(t).start()
+        across_q(t, 0).start()
+        across_q(t, 1).start()
     send_before(0)
     weight(0, 0).start()
 
@@ -304,7 +306,10 @@
         )
         here = pl.ds(pl.multiple_of(t * TILE, TILE), TILE)
         window = pl.ds(pl.multiple_of(t * TILE, TILE), 3 * TILE)
-        for h in range(width // HD):
+        heads = width // HD
+        for h in range(heads):
+            if j == 1 and h % (heads // 2) == 0:
+                across_q(t, h // (heads // 2)).wait_recv()
             span = slice(h * HD, (h + 1) * HD)
             kv = slice(h // group * HD, (h // group + 1) * HD)
             scores = lax.dot_general(
@@ -327,12 +332,10 @@
 
     relay_direct(0)
     wait_before(1)
-    across_q(0).wait_recv()
     attend(1, 0)
     relay_direct(1)
     relay_plane(0)
     for t in range(1, tiles):
-        across_q(t).wait_recv()
         attend(1, t)
     relay_direct(2)
 
@@ -377,7 +380,8 @@
     across(0).wait_send()
     across(1).wait_send()
     for t in range(tiles):
-        across_q(t).wait_send()
+        across_q(t, 0).wait_send()
+        across_q(t, 1).wait_send()
     sent_before(0)
     sent_before(1)
 
@@ -414,8 +418,8 @@
             pltpu.VMEM((rows, n_out), jnp.float32),
             pltpu.VMEM((rows, n_out), bf16),
             dma((4,)),
-            dma((2 + rows // TILE,)),
-            dma((2 + rows // TILE,)),
+            dma((2 + 2 * rows // TILE,)),
+            dma((2 + 2 * rows // TILE,)),
             dma((2, 2)),
             dma((2, 2)),
             dma((4, PAIRS)),
@@ -424,7 +428,7 @@
             dma((PAIRS,)),
         ],
         compiler_params=pltpu.CompilerParams(
-            collective_id=0, has_side_effects=True, vmem_limit_bytes=44 * 1024 * 1024
+            collective_id=0, has_side_effects=True, vmem_limit_bytes=50 * 1024 * 1024
         ),
     )(queries, keys, values, segments.reshape(-1, TILE), out_weight)
 

time: 98.6 us -> 97.2 us (0.986)
  local copies, waits for them, and re-layouts: 5.57 us -> 3.98 us
    unnamed x9 -> x7, local copies, waits for them, and re-layouts: 5.57 us -> 3.98 us
where the time goes in v4:
time: 97.2 us; the launch traced here: 97 us
  Pallas kernels  93 us (96%)
  local copies, waits for them, and re-layouts  3.98 us (4%)
    pallas_call x1, Pallas kernels, square_shards(): pl.pallas_call(functools.partial(kernel, n_seq), out_shape=jax.ShapeDtype...  93 us
    unnamed x7, local copies, waits for them, and re-layouts  3.98 us

profile of v4, /device:TPU:0, one launch (start us, length us, event | category | flops | bytes accessed | tf_op | source)
XLA Modules:
  0.0 97.0 jit_solution(1278067819053809631)
XLA Ops:
  0.0 0.0 copy-start
  0.0 0.9 copy-done
  1.0 0.0 copy-start.1
  1.0 0.9 copy-done.1
  1.9 0.0 copy-start.2
  1.9 0.8 copy-done.2
  2.7 93.0 %shard_map.55 = bf16[256,4096]{1,0:T(8,128)(2,1)S(1)} custom-call(bf16[256,4096]{1,0:T(8,128)(2,1)} %q_hbm.1, bf16[256,512]{1,0:T(8,128)(2,1)S(1)} %copy-done, bf16[256,512]{1,0:T(8,128)(2,1)S(1)} %copy-done.1, s32[64,128]{1,0:T(8,128)S(1)} %bitcast.1, bf16[1024,4096]{1,0:T(8,128)(2,1)} %w_hbm.1), custom_call_target="tpu_custom_call" | custom-call | tf_op jit(solution)/shard_map/pallas_call | solution.py:404
  95.7 1.3 %copy.7 = bf16[256,4096]{1,0:T(8,128)(2,1)} copy(bf16[256,4096]{1,0:T(8,128)(2,1)S(1)} %shard_map.55) | data formatting | bytes 4194304
Async XLA Ops:
  0.0 0.9 copy-start
  1.0 0.9 copy-start.1
  1.9 0.8 copy-start.2

commit v5 on v4

--- a/solution.py
+++ b/solution.py
@@ -361,15 +361,15 @@
         at = cols(i, pair_cols)
         part[:, at] = product(1, at).astype(bf16)
         outward(i).start()
+        @pl.when(i + 1 < PAIRS)
+        def _():
+            relay_plane(i + 1)
+
+        @pl.when(i + 3 < PAIRS)
+        def _():
+            relay_direct(i + 3)
+
         own[:, at] = product(0, at)
-
-        @pl.when(i + 1 < PAIRS)
-        def _():
-            relay_plane(i + 1)
-
-        @pl.when(i + 3 < PAIRS)
-        def _():
-            relay_direct(i + 3)
 
     @pl.loop(0, PAIRS)
     def _(i):

time: 97.2 us -> 97.2 us (level)
  no operation moved by 1% of the time
where the time goes in v5:
time: 97.2 us; the launch traced here: 97 us
  Pallas kernels  93 us (96%)
  local copies, waits for them, and re-layouts  3.98 us (4%)
    pallas_call x1, Pallas kernels, square_shards(): pl.pallas_call(functools.partial(kernel, n_seq), out_shape=jax.ShapeDtype...  93 us
    unnamed x7, local copies, waits for them, and re-layouts  3.98 us

profile of v5, /device:TPU:0, one launch (start us, length us, event | category | flops | bytes accessed | tf_op | source)
XLA Modules:
  0.0 97.0 jit_solution(15089005998668236844)
XLA Ops:
  0.0 0.0 copy-start
  0.0 0.9 copy-done
  1.0 0.0 copy-start.1
  1.0 0.9 copy-done.1
  1.9 0.0 copy-start.2
  1.9 0.8 copy-done.2
  2.7 93.0 %shard_map.55 = bf16[256,4096]{1,0:T(8,128)(2,1)S(1)} custom-call(bf16[256,4096]{1,0:T(8,128)(2,1)} %q_hbm.1, bf16[256,512]{1,0:T(8,128)(2,1)S(1)} %copy-done, bf16[256,512]{1,0:T(8,128)(2,1)S(1)} %copy-done.1, s32[64,128]{1,0:T(8,128)S(1)} %bitcast.1, bf16[1024,4096]{1,0:T(8,128)(2,1)} %w_hbm.1), custom_call_target="tpu_custom_call" | custom-call | tf_op jit(solution)/shard_map/pallas_call | solution.py:404
  95.7 1.3 %copy.7 = bf16[256,4096]{1,0:T(8,128)(2,1)} copy(bf16[256,4096]{1,0:T(8,128)(2,1)S(1)} %shard_map.55) | data formatting | bytes 4194304
Async XLA Ops:
  0.0 0.9 copy-start
  1.0 0.9 copy-start.1
  1.9 0.8 copy-start.2
